TPU v7x, 32 devices: a whole 2x2x4 slice. The times are simulated.
32 devices in a mesh: lat: 4 (over y, x), lon: 8 (over z, core).
Axes of the slice: x: 2, y: 2, z: 4, core: 2. Of those that a mesh axis runs over, the one named last changes fastest.
Arguments:
- ensemble: bfloat16 [32, 32, 10240], P('lon', 'lat'), may hold values from -0.625 to 0.625
- innovation: float32 [64, 64, 128], P('lon', 'lat'), may hold values from -6 to 6
- obs_weight: float32 [64, 64, 128], P('lon', 'lat'), may hold values from 0.5 to 20
- lat_offset: int32 [64], P('lat'), may hold values from 0 to 3
- lat_weight: float32 [64], P('lat'), may hold values from 0 to 1
- band_widths: int32 [80], replicated, may hold values from 1 to 63
Outputs:
- coefficients: float32 [2, 2], replicated
- next_vector: bfloat16 [32, 32, 5120], P('lon', 'lat')
All inputs are finite; a program needn't handle non-finite values.
Results may differ from a plain program's by a relative error of at most 0.0014.
Values sent between devices are 32-bit elements; how exact they have to be, the bound alone decides.
No kernel may reach another device: no remote copies, remote signals or barrier semaphores. Data moves between devices by JAX's collectives and lax.ppermute only.
A program may use at most 64 MiB of HBM per device.

v0:
```python
import jax
import jax.numpy as jnp
from jax import lax
from jax.sharding import PartitionSpec as P

M = 80
LEV = 64
FIELDS = 2
ITERS = 2
EVEN_TAPS = (-0.0234375, 0.2265625, 0.8671875, -0.0703125)
ODD_TAPS = (-0.0703125, 0.8671875, 0.2265625, -0.0234375)
EPSILON = 1e-06


def padded_2(block, sides, width, periodic):
    for axis, dim in sides:
        count = lax.axis_size(axis)
        forward = [(i, i + 1) for i in range(count - 1)]
        if periodic:
            forward.append((count - 1, 0))
        backward = [(target, source) for source, target in forward]
        low = lax.ppermute(
            lax.slice_in_dim(block, block.shape[dim] - width, None, axis=dim), axis, forward
        )
        high = lax.ppermute(lax.slice_in_dim(block, 0, width, axis=dim), axis, backward)
        block = jnp.concatenate([low, block, high], axis=dim)
    return block


def tent_matrix(band_widths, levels):
    level_ids = jnp.arange(levels, dtype=jnp.int32)
    distance = jnp.abs(level_ids[:, None] - level_ids[None, :]).astype(jnp.float32)
    widths = (band_widths + 1).astype(jnp.float32)[:, None, None]
    return jnp.maximum(0.0, 1.0 - distance[None] / widths) / widths


def tap_sum(padded, taps, first, length):
    result = taps[0] * padded[first : first + length]
    for offset in range(1, 4):
        result = result + taps[offset] * padded[first + offset : first + offset + length]
    return result


def fold_taps(padded, taps, first, length):
    result = taps[0] * padded[first : first + 2 * length : 2]
    for offset in range(1, 4):
        start_at = first - 2 * offset
        result = result + taps[offset] * padded[start_at : start_at + 2 * length : 2]
    return result


def localize(values, tent):
    lon_cols, lat_rows = (values.shape[0], values.shape[1])
    shaped = values.reshape(lon_cols, lat_rows, M, LEV)
    mapped = jnp.einsum("abml,mlk->abmk", shaped, tent, precision=lax.Precision.HIGHEST)
    return mapped.reshape(lon_cols, lat_rows, M * LEV)


def settle_rows(gathered, lat_rows):
    lon_cols, columns_all = (gathered.shape[0], gathered.shape[2])
    zeros_mid = jnp.zeros((lon_cols, lat_rows - 4, columns_all), jnp.float32)
    rim_out = jnp.concatenate([gathered[:, :2], zeros_mid, gathered[:, lat_rows + 2 :]], axis=1)
    rim_in = padded_2(rim_out, (("lat", 1),), 2, False)
    return gathered[:, 2 : lat_rows + 2] + jnp.concatenate(
        [rim_in[:, :2], zeros_mid, rim_in[:, lat_rows + 2 :]], axis=1
    )


def per_device(ensemble, innovation, obs_weight, lat_offset, lat_weight, band_widths):
    lon_cols, lat_rows = (ensemble.shape[0], ensemble.shape[1])
    fine_cols, fine_rows = (innovation.shape[0], innovation.shape[1])
    columns_all = innovation.shape[2]
    tent = tent_matrix(band_widths, LEV)
    row_ids = jnp.arange(fine_rows, dtype=jnp.int32)
    lower = row_ids // 2 + lat_offset
    columns = jnp.arange(lat_rows + 4, dtype=jnp.int32)
    interp = (1.0 - lat_weight)[:, None] * (columns[None, :] == lower[:, None]) + lat_weight[
        :, None
    ] * (columns[None, :] == lower[:, None] + 1)
    entries = float(lon_cols * lat_rows * M * LEV * lax.axis_size("lat") * lax.axis_size("lon"))
    position = lax.axis_index("lat")
    keep_rows = (
        ((columns >= 2) | (position > 0))
        & ((columns < lat_rows + 2) | (position < lax.axis_size("lat") - 1))
    ).astype(jnp.float32)

    def spread(coarse):
        shaped = ensemble.reshape(lon_cols, lat_rows, M, FIELDS, LEV)
        summed = jnp.sum(shaped * coarse.reshape(lon_cols, lat_rows, 1, FIELDS, LEV), axis=3)
        return localize(summed.reshape(lon_cols, lat_rows, M * LEV), tent)

    def restrict(fine):
        padded = padded_2(fine, (("lon", 0),), 3, True)
        coarse_lon = fold_taps(padded, EVEN_TAPS, 7, lon_cols) + fold_taps(
            padded, ODD_TAPS, 6, lon_cols
        )
        gathered = jnp.einsum("ri,crl->cil", interp, coarse_lon, precision=lax.Precision.HIGHEST)
        return settle_rows(gathered, lat_rows)

    current = spread(restrict(obs_weight * innovation))
    basis = []
    diagonal = []
    off_diagonal = []
    for step in range(ITERS):
        weights = localize(current, tent)
        combine_shaped = ensemble.reshape(lon_cols, lat_rows, M, FIELDS, LEV)
        combine_summed = jnp.sum(
            combine_shaped * weights.reshape(lon_cols, lat_rows, M, 1, LEV), axis=2
        )
        prolong_padded = padded_2(
            combine_summed.reshape(lon_cols, lat_rows, FIELDS * LEV),
            (("lat", 1), ("lon", 0)),
            2,
            True,
        )
        prolong_padded = prolong_padded * keep_rows[None, :, None]
        fine_lat = jnp.einsum(
            "ri,cil->crl", interp, prolong_padded, precision=lax.Precision.HIGHEST
        )
        even_cols = tap_sum(fine_lat, EVEN_TAPS, 0, lon_cols)
        odd_cols = tap_sum(fine_lat, ODD_TAPS, 1, lon_cols)
        image_raw = current + spread(
            restrict(
                obs_weight
                * jnp.stack([even_cols, odd_cols], axis=1).reshape(
                    fine_cols, fine_rows, columns_all
                )
            )
        )
        local_dots = jnp.stack(
            [jnp.sum(member * image_raw) for member in basis]
            + [jnp.sum(current * image_raw), jnp.sum(current * current)]
        )
        sums_all = lax.psum(local_dots, ("lat", "lon"))
        norm_value = jnp.sqrt(sums_all[-1] / entries + EPSILON)
        normed = current / norm_value
        image = image_raw / norm_value
        dots = jnp.concatenate(
            [
                sums_all[:-2] / (entries * norm_value),
                sums_all[-2:-1] / (entries * norm_value * norm_value),
            ]
        )
        basis.append(normed)
        for which_one, member in enumerate(basis):
            image = image - dots[which_one] * member
        diagonal.append(dots[-1])
        off_diagonal.append(norm_value)
        current = image
    coefficients = jnp.stack([jnp.stack(diagonal), jnp.stack(off_diagonal)])
    return (coefficients, current.astype(jnp.bfloat16))


def solution(mesh):
    return jax.shard_map(
        per_device,
        mesh=mesh,
        in_specs=(
            P("lon", "lat", None),
            P("lon", "lat", None),
            P("lon", "lat", None),
            P("lat"),
            P("lat"),
            P(),
        ),
        out_specs=(P(), P("lon", "lat", None)),
        check_vma=False,
    )
```

profile of v0, /device:TPU:10, one launch (start us, length us, event | category | flops | bytes accessed | tf_op | source)
XLA Modules:
  0.0 196.6 jit_solution(7050286283298592275)
XLA Ops:
  6.2 3.4 %collective-permute-start.2 = (f32[4,2,128]{2,1,0:T(2,128)S(1)}, f32[4,2,128]{2,1,0:T(2,128)S(1)}, u32[]{:S(2)}, u32[]{:S(2)}) collective-permute-start(f32[4,2,128]{2,1,0:T(2,128)S(1)} %get-tuple-element.27), channel_id=1, source_target_pairs={{0,8},{8,16},{16,24},{1,9},{9,17},{17,25},{2,10},{10,18},{18,26},{... | collective-permute-start | bytes 12296 | tf_op jit(solution)/shard_map/ppermute | solution.py:22
  9.6 2.4 %collective-permute-start.3 = (f32[4,2,128]{2,1,0:T(2,128)S(1)}, f32[4,2,128]{2,1,0:T(2,128)S(1)}, u32[]{:S(2)}, u32[]{:S(2)}) collective-permute-start(f32[4,2,128]{2,1,0:T(2,128)S(1)} %get-tuple-element.28), channel_id=1, source_target_pairs={{8,0},{16,8},{24,16},{9,1},{17,9},{25,17},{10,2},{18,10},{26,18},{... | collective-permute-start | bytes 12296 | tf_op jit(solution)/shard_map/ppermute | solution.py:25
  12.1 3.5 %reshape.94 = f32[4,8,80,2,64]{4,3,2,1,0:T(2,128)S(1)} reshape(bf16[4,8,10240]{2,1,0:T(8,128)(2,1)} %param.6) | data formatting | bytes 1966080 | tf_op jit(solution)/shard_map/convert_element_type | solution.py:89
  16.2 3.8 %multiply_reduce_fusion.4 = f32[4,8,80,64]{3,2,1,0:T(8,128)S(1)} fusion(f32[4,8,80,2,64]{4,3,2,1,0:T(2,128)S(1)} %reshape.94, f32[4,8,2,64]{3,2,1,0:T(2,128)S(1)} %mul.273), kind=kLoop, calls=%fused_computation.7 | loop fusion | flops 491520 | bytes 1982464 | tf_op jit(solution)/shard_map/reduce_sum | solution.py:89
  20.0 3.0 %fusion.8 = f32[80,64,32]{1,2,0:S(1)} fusion(f32[4,8,80,64]{3,2,1,0:T(8,128)S(1)} %multiply_reduce_fusion.4, f32[80]{0:T(128)S(1)} %add_convert_fusion, f32[64,64]{1,0:T(8,128)S(1)} %abs_convert_fusion), kind=kOutput, calls=%fused_computation.18 | convolution fusion | flops 127139840 | bytes 1327424
  23.1 2.8 %convolution_bitcast_fusion.3 = f32[4,8,80,64]{3,1,0,2:T(8,128)S(1)} fusion(f32[80,64,32]{1,2,0:S(1)} %fusion.8, f32[80]{0:T(128)S(1)} %add_convert_fusion, f32[64,64]{1,0:T(8,128)S(1)} %abs_convert_fusion), kind=kOutput, calls=%fused_computation.11 | convolution fusion | flops 127139840 | bytes 1327424
  26.7 2.0 multiply_reduce_fusion.3
  28.8 2.1 %collective-permute-start.4 = (f32[4,2,128]{2,1,0:T(2,128)S(1)}, f32[4,2,128]{2,1,0:T(2,128)S(1)}, u32[]{:S(2)}, u32[]{:S(2)}) collective-permute-start(f32[4,2,128]{2,1,0:T(2,128)S(1)} %get-tuple-element.31), channel_id=1, source_target_pairs={{0,8},{8,16},{16,24},{24,0},{1,9},{9,17},{17,25},{25,1},{2,10},{10... | collective-permute-start | bytes 12296 | tf_op jit(solution)/shard_map/ppermute | solution.py:22
  32.4 2.9 %collective-permute-done.5 = f32[4,2,128]{2,1,0:T(2,128)S(1)} collective-permute-done((f32[4,2,128]{2,1,0:T(2,128)S(1)}, f32[4,2,128]{2,1,0:T(2,128)S(1)}, u32[]{:S(2)}, u32[]{:S(2)}) %collective-permute-start.5) | collective-permute-done | bytes 4128 | tf_op jit(solution)/shard_map/ppermute | solution.py:25
  42.6 1.9 collective-permute-start.10
  44.5 3.9 %collective-permute-start.11 = (f32[4,2,128]{2,1,0:T(2,128)S(1)}, f32[4,2,128]{2,1,0:T(2,128)S(1)}, u32[]{:S(2)}, u32[]{:S(2)}) collective-permute-start(f32[4,2,128]{2,1,0:T(2,128)S(1)} %get-tuple-element.24), channel_id=1, source_target_pairs={{8,0},{16,8},{24,16},{9,1},{17,9},{25,17},{10,2},{18,10},{26,18},{... | collective-permute-start | bytes 12296 | tf_op jit(solution)/shard_map/ppermute | solution.py:25
  48.4 2.5 %collective-permute-done.11 = f32[4,2,128]{2,1,0:T(2,128)S(1)} collective-permute-done((f32[4,2,128]{2,1,0:T(2,128)S(1)}, f32[4,2,128]{2,1,0:T(2,128)S(1)}, u32[]{:S(2)}, u32[]{:S(2)}) %collective-permute-start.11) | collective-permute-done | bytes 4128 | tf_op jit(solution)/shard_map/ppermute | solution.py:25
  51.1 3.8 %multiply_reduce_fusion.2 = f32[4,8,80,64]{3,2,1,0:T(8,128)S(1)} fusion(f32[4,8,80,2,64]{4,3,2,1,0:T(2,128)S(1)} %reshape.94, f32[4,8,2,64]{3,2,1,0:T(2,128)S(1)} %mul.296), kind=kLoop, calls=%fused_computation.5 | loop fusion | flops 491520 | bytes 1982464 | tf_op jit(solution)/shard_map/reduce_sum | solution.py:89
  54.9 4.8 %fusion.10 = (f32[]{:T(128)}, f32[]{:T(128)}, f32[4,8,80,64]{3,1,0,2:T(8,128)}) fusion(f32[80,64,32]{1,2,0:S(1)} %copy-done.1, f32[4,8,80,64]{3,2,1,0:T(8,128)S(1)} %multiply_reduce_fusion.2, f32[80]{0:T(128)S(1)} %add_convert_fusion, f32[64,64]{1,0:T(8,128)S(1)} %abs_convert_fusion), kind=kOutput, calls=%fused_computation.23 | convolution fusion | flops 127959040 | bytes 1982792
  61.1 45.0 %psum.14 = f32[2]{0:T(128)S(1)} all-reduce(f32[2]{0:T(128)S(1)} %pad_maximum_fusion.8), channel_id=1, replica_groups=mesh['lat'=4,'lon'=8] {'lat','lon'}, use_global_device_ids=true, to_apply=%region_5.6 | all-reduce | flops 2 | bytes 16 | tf_op jit(solution)/shard_map/psum | solution.py:134
  108.0 4.7 %convolution_bitcast_fusion.1 = f32[4,8,80,64]{3,1,0,2:T(8,128)S(1)} fusion(f32[80]{0:T(128)S(1)} %add_convert_fusion, f32[64,64]{1,0:T(8,128)S(1)} %abs_convert_fusion, f32[4,8,80,64]{3,1,0,2:T(8,128)} %get-tuple-element.38, f32[]{:T(128)} %bitcast.25, f32[]{:T(128)} %bitcast.23, f32[80,64,32]{1,2,0} %copy-done), kind=kOutput, calls=%fused_computation.9 | convolution fusion | flops 127795200 | bytes 1982792
  118.7 2.4 %collective-permute-done.13 = f32[4,2,128]{2,1,0:T(2,128)S(1)} collective-permute-done((f32[4,2,128]{2,1,0:T(2,128)S(1)}, f32[4,2,128]{2,1,0:T(2,128)S(1)}, u32[]{:S(2)}, u32[]{:S(2)}) %collective-permute-start.13) | collective-permute-done | bytes 4128 | tf_op jit(solution)/shard_map/ppermute | solution.py:25
  128.3 1.9 collective-permute-start.18
  130.2 4.1 %collective-permute-start.19 = (f32[4,2,128]{2,1,0:T(2,128)S(1)}, f32[4,2,128]{2,1,0:T(2,128)S(1)}, u32[]{:S(2)}, u32[]{:S(2)}) collective-permute-start(f32[4,2,128]{2,1,0:T(2,128)S(1)} %get-tuple-element.20), channel_id=1, source_target_pairs={{8,0},{16,8},{24,16},{9,1},{17,9},{25,17},{10,2},{18,10},{26,18},{... | collective-permute-start | bytes 12296 | tf_op jit(solution)/shard_map/ppermute | solution.py:25
  134.4 2.3 %collective-permute-done.19 = f32[4,2,128]{2,1,0:T(2,128)S(1)} collective-permute-done((f32[4,2,128]{2,1,0:T(2,128)S(1)}, f32[4,2,128]{2,1,0:T(2,128)S(1)}, u32[]{:S(2)}, u32[]{:S(2)}) %collective-permute-start.19) | collective-permute-done | bytes 4128 | tf_op jit(solution)/shard_map/ppermute | solution.py:25
  136.8 3.8 %multiply_reduce_fusion = f32[4,8,80,64]{3,2,1,0:T(8,128)S(1)} fusion(f32[4,8,80,2,64]{4,3,2,1,0:T(2,128)S(1)} %reshape.94, f32[4,8,2,64]{3,2,1,0:T(2,128)S(1)} %mul.324), kind=kLoop, calls=%fused_computation.3 | loop fusion | flops 491520 | bytes 1982464 | tf_op jit(solution)/shard_map/reduce_sum | solution.py:89
  140.7 5.1 %multiply_reduce_fusion.7 = (f32[]{:T(128)}, f32[]{:T(128)}, f32[]{:T(128)}, f32[4,8,80,64]{3,1,0,2:T(8,128)}) fusion(f32[]{:T(128)} %bitcast.23, f32[80,64,32]{1,2,0:S(1)} %copy-done.2, f32[4,8,80,64]{3,2,1,0:T(8,128)S(1)} %multiply_reduce_fusion, f32[80]{0:T(128)S(1)} %add_convert_fusion, f32[64,64]{1,0:T(8,128)S(1)} %abs_convert_fusion, f32[]{:T(128)} %bitcast.25, ...), kind=kOutput, calls=%fused_computation.31 | convolution fusion | flops 128942080 | bytes 2638164
  145.8 2.1 %pad_maximum_fusion.9 = f32[3]{0:T(128)S(1)} fusion(f32[1]{0:T(128)} %bitcast.42, f32[1]{0:T(128)} %bitcast.41, f32[1]{0:T(128)} %bitcast.40), kind=kLoop, calls=%fused_computation.211 | loop fusion | flops 6 | bytes 24 | tf_op jit(solution)/shard_map/stack | solution.py:130
  147.9 41.9 %psum.15 = f32[3]{0:T(128)S(1)} all-reduce(f32[3]{0:T(128)S(1)} %pad_maximum_fusion.9), channel_id=1, replica_groups=mesh['lat'=4,'lon'=8] {'lat','lon'}, use_global_device_ids=true, to_apply=%region_11.12 | all-reduce | flops 3 | bytes 24 | tf_op jit(solution)/shard_map/psum | solution.py:134
  (100 shorter events, 35.6 us)
Async XLA Ops:
  1.5 3.8 %collective-permute-start = (f32[3,16,128]{2,1,0:T(8,128)S(1)}, f32[3,16,128]{2,1,0:T(8,128)S(1)}, u32[]{:S(2)}, u32[]{:S(2)}) collective-permute-start(f32[3,16,128]{2,1,0:T(8,128)S(1)} %get-tuple-element.17), channel_id=1, source_target_pairs={{0,1},{1,2},{2,3},{3,4},{4,5},{5,6},{6,7},{7,0},{8,9},{9,10},{10,1... | collective-permute-start | bytes 73736 | tf_op jit(solution)/shard_map/ppermute | solution.py:22
  1.6 3.7 %collective-permute-start.1 = (f32[3,16,128]{2,1,0:T(8,128)S(1)}, f32[3,16,128]{2,1,0:T(8,128)S(1)}, u32[]{:S(2)}, u32[]{:S(2)}) collective-permute-start(f32[3,16,128]{2,1,0:T(8,128)S(1)} %get-tuple-element.18), channel_id=1, source_target_pairs={{1,0},{2,1},{3,2},{4,3},{5,4},{6,5},{7,6},{0,7},{9,8},{10,9},{11,1... | collective-permute-start | bytes 73736 | tf_op jit(solution)/shard_map/ppermute | solution.py:25
  6.2 9.4 %collective-permute-start.2 = (f32[4,2,128]{2,1,0:T(2,128)S(1)}, f32[4,2,128]{2,1,0:T(2,128)S(1)}, u32[]{:S(2)}, u32[]{:S(2)}) collective-permute-start(f32[4,2,128]{2,1,0:T(2,128)S(1)} %get-tuple-element.27), channel_id=1, source_target_pairs={{0,8},{8,16},{16,24},{1,9},{9,17},{17,25},{2,10},{10,18},{18,26},{... | collective-permute-start | bytes 12296 | tf_op jit(solution)/shard_map/ppermute | solution.py:22
  9.6 6.4 %collective-permute-start.3 = (f32[4,2,128]{2,1,0:T(2,128)S(1)}, f32[4,2,128]{2,1,0:T(2,128)S(1)}, u32[]{:S(2)}, u32[]{:S(2)}) collective-permute-start(f32[4,2,128]{2,1,0:T(2,128)S(1)} %get-tuple-element.28), channel_id=1, source_target_pairs={{8,0},{16,8},{24,16},{9,1},{17,9},{25,17},{10,2},{18,10},{26,18},{... | collective-permute-start | bytes 12296 | tf_op jit(solution)/shard_map/ppermute | solution.py:25
  26.7 11.9 %copy-start.7 = (f32[16]{0:T(128)S(1)}, f32[16]{0:T(128)}, u32[]{:S(2)}) copy-start(f32[16]{0:T(128)} %param.10) | copy-start | bytes 196
  26.7 12.2 %copy-start.6 = (f32[8,16,128]{2,1,0:T(8,128)S(1)}, f32[8,16,128]{2,1,0:T(8,128)}, u32[]{:S(2)}) copy-start(f32[8,16,128]{2,1,0:T(8,128)} %param.8) | copy-start | bytes 196612
  28.8 3.6 %collective-permute-start.4 = (f32[4,2,128]{2,1,0:T(2,128)S(1)}, f32[4,2,128]{2,1,0:T(2,128)S(1)}, u32[]{:S(2)}, u32[]{:S(2)}) collective-permute-start(f32[4,2,128]{2,1,0:T(2,128)S(1)} %get-tuple-element.31), channel_id=1, source_target_pairs={{0,8},{8,16},{16,24},{24,0},{1,9},{9,17},{17,25},{25,1},{2,10},{10... | collective-permute-start | bytes 12296 | tf_op jit(solution)/shard_map/ppermute | solution.py:22
  30.8 4.5 %collective-permute-start.5 = (f32[4,2,128]{2,1,0:T(2,128)S(1)}, f32[4,2,128]{2,1,0:T(2,128)S(1)}, u32[]{:S(2)}, u32[]{:S(2)}) collective-permute-start(f32[4,2,128]{2,1,0:T(2,128)S(1)} %get-tuple-element.32), channel_id=1, source_target_pairs={{8,0},{16,8},{24,16},{0,24},{9,1},{17,9},{25,17},{1,25},{10,2},{18... | collective-permute-start | bytes 12296 | tf_op jit(solution)/shard_map/ppermute | solution.py:25
  35.4 3.2 %collective-permute-start.6 = (f32[2,12,128]{2,1,0:T(8,128)S(1)}, f32[2,12,128]{2,1,0:T(8,128)S(1)}, u32[]{:S(2)}, u32[]{:S(2)}) collective-permute-start(f32[2,12,128]{2,1,0:T(8,128)S(1)} %get-tuple-element.25), channel_id=1, source_target_pairs={{0,1},{1,2},{2,3},{3,4},{4,5},{5,6},{6,7},{7,0},{8,9},{9,10},{10,1... | collective-permute-start | bytes 36872 | tf_op jit(solution)/shard_map/ppermute | solution.py:22
  35.4 3.2 %collective-permute-start.7 = (f32[2,12,128]{2,1,0:T(8,128)S(1)}, f32[2,12,128]{2,1,0:T(8,128)S(1)}, u32[]{:S(2)}, u32[]{:S(2)}) collective-permute-start(f32[2,12,128]{2,1,0:T(8,128)S(1)} %get-tuple-element.26), channel_id=1, source_target_pairs={{1,0},{2,1},{3,2},{4,3},{5,4},{6,5},{7,6},{0,7},{9,8},{10,9},{11,1... | collective-permute-start | bytes 36872 | tf_op jit(solution)/shard_map/ppermute | solution.py:25
  39.0 3.3 %collective-permute-start.8 = (f32[3,16,128]{2,1,0:T(8,128)S(1)}, f32[3,16,128]{2,1,0:T(8,128)S(1)}, u32[]{:S(2)}, u32[]{:S(2)}) collective-permute-start(f32[3,16,128]{2,1,0:T(8,128)S(1)} %get-tuple-element.13), channel_id=1, source_target_pairs={{0,1},{1,2},{2,3},{3,4},{4,5},{5,6},{6,7},{7,0},{8,9},{9,10},{10,1... | collective-permute-start | bytes 73736 | tf_op jit(solution)/shard_map/ppermute | solution.py:22
  40.7 1.6 collective-permute-start.9
  42.6 5.9 %collective-permute-start.10 = (f32[4,2,128]{2,1,0:T(2,128)S(1)}, f32[4,2,128]{2,1,0:T(2,128)S(1)}, u32[]{:S(2)}, u32[]{:S(2)}) collective-permute-start(f32[4,2,128]{2,1,0:T(2,128)S(1)} %get-tuple-element.23), channel_id=1, source_target_pairs={{0,8},{8,16},{16,24},{1,9},{9,17},{17,25},{2,10},{10,18},{18,26},{... | collective-permute-start | bytes 12296 | tf_op jit(solution)/shard_map/ppermute | solution.py:22
  44.5 6.4 %collective-permute-start.11 = (f32[4,2,128]{2,1,0:T(2,128)S(1)}, f32[4,2,128]{2,1,0:T(2,128)S(1)}, u32[]{:S(2)}, u32[]{:S(2)}) collective-permute-start(f32[4,2,128]{2,1,0:T(2,128)S(1)} %get-tuple-element.24), channel_id=1, source_target_pairs={{8,0},{16,8},{24,16},{9,1},{17,9},{25,17},{10,2},{18,10},{26,18},{... | collective-permute-start | bytes 12296 | tf_op jit(solution)/shard_map/ppermute | solution.py:25
  115.1 3.6 %collective-permute-start.12 = (f32[4,2,128]{2,1,0:T(2,128)S(1)}, f32[4,2,128]{2,1,0:T(2,128)S(1)}, u32[]{:S(2)}, u32[]{:S(2)}) collective-permute-start(f32[4,2,128]{2,1,0:T(2,128)S(1)} %get-tuple-element.29), channel_id=1, source_target_pairs={{0,8},{8,16},{16,24},{24,0},{1,9},{9,17},{17,25},{25,1},{2,10},{10... | collective-permute-start | bytes 12296 | tf_op jit(solution)/shard_map/ppermute | solution.py:22
  116.6 4.5 %collective-permute-start.13 = (f32[4,2,128]{2,1,0:T(2,128)S(1)}, f32[4,2,128]{2,1,0:T(2,128)S(1)}, u32[]{:S(2)}, u32[]{:S(2)}) collective-permute-start(f32[4,2,128]{2,1,0:T(2,128)S(1)} %get-tuple-element.30), channel_id=1, source_target_pairs={{8,0},{16,8},{24,16},{0,24},{9,1},{17,9},{25,17},{1,25},{10,2},{18... | collective-permute-start | bytes 12296 | tf_op jit(solution)/shard_map/ppermute | solution.py:25
  121.1 3.2 %collective-permute-start.14 = (f32[2,12,128]{2,1,0:T(8,128)S(1)}, f32[2,12,128]{2,1,0:T(8,128)S(1)}, u32[]{:S(2)}, u32[]{:S(2)}) collective-permute-start(f32[2,12,128]{2,1,0:T(8,128)S(1)} %get-tuple-element.21), channel_id=1, source_target_pairs={{0,1},{1,2},{2,3},{3,4},{4,5},{5,6},{6,7},{7,0},{8,9},{9,10},{10,1... | collective-permute-start | bytes 36872 | tf_op jit(solution)/shard_map/ppermute | solution.py:22
  121.2 3.2 %collective-permute-start.15 = (f32[2,12,128]{2,1,0:T(8,128)S(1)}, f32[2,12,128]{2,1,0:T(8,128)S(1)}, u32[]{:S(2)}, u32[]{:S(2)}) collective-permute-start(f32[2,12,128]{2,1,0:T(8,128)S(1)} %get-tuple-element.22), channel_id=1, source_target_pairs={{1,0},{2,1},{3,2},{4,3},{5,4},{6,5},{7,6},{0,7},{9,8},{10,9},{11,1... | collective-permute-start | bytes 36872 | tf_op jit(solution)/shard_map/ppermute | solution.py:25
  124.7 3.3 %collective-permute-start.16 = (f32[3,16,128]{2,1,0:T(8,128)S(1)}, f32[3,16,128]{2,1,0:T(8,128)S(1)}, u32[]{:S(2)}, u32[]{:S(2)}) collective-permute-start(f32[3,16,128]{2,1,0:T(8,128)S(1)} %get-tuple-element.9), channel_id=1, source_target_pairs={{0,1},{1,2},{2,3},{3,4},{4,5},{5,6},{6,7},{7,0},{8,9},{9,10},{10,1... | collective-permute-start | bytes 73736 | tf_op jit(solution)/shard_map/ppermute | solution.py:22
  125.6 2.5 %collective-permute-start.17 = (f32[3,16,128]{2,1,0:T(8,128)S(1)}, f32[3,16,128]{2,1,0:T(8,128)S(1)}, u32[]{:S(2)}, u32[]{:S(2)}) collective-permute-start(f32[3,16,128]{2,1,0:T(8,128)S(1)} %get-tuple-element.10), channel_id=1, source_target_pairs={{1,0},{2,1},{3,2},{4,3},{5,4},{6,5},{7,6},{0,7},{9,8},{10,9},{11,1... | collective-permute-start | bytes 73736 | tf_op jit(solution)/shard_map/ppermute | solution.py:25
  128.3 6.1 %collective-permute-start.18 = (f32[4,2,128]{2,1,0:T(2,128)S(1)}, f32[4,2,128]{2,1,0:T(2,128)S(1)}, u32[]{:S(2)}, u32[]{:S(2)}) collective-permute-start(f32[4,2,128]{2,1,0:T(2,128)S(1)} %get-tuple-element.19), channel_id=1, source_target_pairs={{0,8},{8,16},{16,24},{1,9},{9,17},{17,25},{2,10},{10,18},{18,26},{... | collective-permute-start | bytes 12296 | tf_op jit(solution)/shard_map/ppermute | solution.py:22
  130.2 6.4 %collective-permute-start.19 = (f32[4,2,128]{2,1,0:T(2,128)S(1)}, f32[4,2,128]{2,1,0:T(2,128)S(1)}, u32[]{:S(2)}, u32[]{:S(2)}) collective-permute-start(f32[4,2,128]{2,1,0:T(2,128)S(1)} %get-tuple-element.20), channel_id=1, source_target_pairs={{8,0},{16,8},{24,16},{9,1},{17,9},{25,17},{10,2},{18,10},{26,18},{... | collective-permute-start | bytes 12296 | tf_op jit(solution)/shard_map/ppermute | solution.py:25
  140.7 51.9 %copy-start.3 = (f32[80,64,32]{1,2,0:S(1)}, f32[80,64,32]{1,2,0}, u32[]{:S(2)}) copy-start(f32[80,64,32]{1,2,0} %copy-done) | copy-start | bytes 1966084
  140.7 51.9 %copy-start.5 = (f32[4,8,80,64]{3,1,0,2:T(8,128)S(1)}, f32[4,8,80,64]{3,1,0,2:T(8,128)}, u32[]{:S(2)}) copy-start(f32[4,8,80,64]{3,1,0,2:T(8,128)} %get-tuple-element.38) | copy-start | bytes 1966084
  (4 other events, 14.4 us)
where the time goes:
time: 200 us; the launch traced here: 197 us
  blocking collectives  86.9 us (43%)
  starting transfers between devices  30.9 us (15%)
  other arithmetic  24 us (12%)
  matrix products  22.2 us (11%)
  waiting for transfers between devices  19.5 us (10%)
  local copies, waits for them, and re-layouts  8.27 us (4%)
  between operations  4.78 us (2%)
    psum x2, blocking collectives, per_device(): sums_all = lax.psum(local_dots, ('lat', 'lon'))  86.9 us
    unnamed x5, matrix products  20.5 us
    ppermute x10, starting transfers between devices, padded_2(): lax.ppermute(lax.slice_in_dim(block, 0, width, axis=dim), axis, backward)  17.3 us
    ppermute x10, starting transfers between devices, padded_2(): lax.ppermute(lax.slice_in_dim(block, block.shape[dim] - width, None, axis...  13.6 us
    reduce_sum x3, other arithmetic, spread(): jnp.sum(shaped * coarse.reshape(lon_cols, lat_rows, 1, FIELDS, LEV), axis=3)  11.5 us
    ppermute x10, waiting for transfers between devices, padded_2(): lax.ppermute(lax.slice_in_dim(block, 0, width, axis=dim), axis, backward)  10.5 us
    ppermute x10, waiting for transfers between devices, padded_2(): lax.ppermute(lax.slice_in_dim(block, block.shape[dim] - width, None, axis...  8.92 us
  transfers between devices with their start and end apart: 20, of which 13 were waited for; matrix products, arithmetic and copies ran while one was open for 3% of the time, Pallas kernels for 0%

commit v1 on v0

--- a/solution.py
+++ b/solution.py
@@ -131,7 +131,7 @@
             [jnp.sum(member * image_raw) for member in basis]
             + [jnp.sum(current * image_raw), jnp.sum(current * current)]
         )
-        sums_all = lax.psum(local_dots, ("lat", "lon"))
+        sums_all = lax.psum(lax.psum(local_dots, "lon"), "lat")
         norm_value = jnp.sqrt(sums_all[-1] / entries + EPSILON)
         normed = current / norm_value
         image = image_raw / norm_value

time: 200 us -> 173 us (0.86)
  the two profiles are of different devices: /device:TPU:10 before, /device:TPU:0 now
where the time goes in v1:
time: 173 us; the launch traced here: 170 us
  blocking collectives  48.8 us (28%)
  starting transfers between devices  42.6 us (25%)
  other arithmetic  24.3 us (14%)
  matrix products  22.2 us (13%)
  waiting for transfers between devices  19.3 us (11%)
  local copies, waits for them, and re-layouts  8.27 us (5%)
  between operations  4.63 us (3%)
    psum x4, blocking collectives, per_device(): sums_all = lax.psum(lax.psum(local_dots, 'lon'), 'lat')  48.8 us
    ppermute x10, starting transfers between devices, padded_2(): lax.ppermute(lax.slice_in_dim(block, 0, width, axis=dim), axis, backward)  25.2 us
    unnamed x5, matrix products  20.5 us
    ppermute x10, starting transfers between devices, padded_2(): lax.ppermute(lax.slice_in_dim(block, block.shape[dim] - width, None, axis...  17.4 us
    reduce_sum x3, other arithmetic, spread(): jnp.sum(shaped * coarse.reshape(lon_cols, lat_rows, 1, FIELDS, LEV), axis=3)  11.5 us
    ppermute x10, waiting for transfers between devices, padded_2(): lax.ppermute(lax.slice_in_dim(block, 0, width, axis=dim), axis, backward)  10.5 us
    ppermute x10, waiting for transfers between devices, padded_2(): lax.ppermute(lax.slice_in_dim(block, block.shape[dim] - width, None, axis...  8.88 us
    convert_element_type x1, local copies, waits for them, and re-layouts, spread(): shaped * coarse.reshape(lon_cols, lat_rows, 1, FIELDS, LEV)  3.48 us
  transfers between devices with their start and end apart: 20, of which 12 were waited for; matrix products, arithmetic and copies ran while one was open for 3% of the time, Pallas kernels for 0%

profile of v1, /device:TPU:0, one launch (start us, length us, event | category | flops | bytes accessed | tf_op | source)
XLA Modules:
  0.0 170.2 jit_solution(16314332300143544638)
XLA Ops:
  2.1 4.1 %collective-permute-start.1 = (f32[3,16,128]{2,1,0:T(8,128)S(1)}, f32[3,16,128]{2,1,0:T(8,128)S(1)}, u32[]{:S(2)}, u32[]{:S(2)}) collective-permute-start(f32[3,16,128]{2,1,0:T(8,128)S(1)} %get-tuple-element.18), channel_id=1, source_target_pairs={{1,0},{2,1},{3,2},{4,3},{5,4},{6,5},{7,6},{0,7},{9,8},{10,9},{11,1... | collective-permute-start | bytes 73736 | tf_op jit(solution)/shard_map/ppermute | solution.py:25
  9.0 3.8 %collective-permute-start.2 = (f32[4,2,128]{2,1,0:T(2,128)S(1)}, f32[4,2,128]{2,1,0:T(2,128)S(1)}, u32[]{:S(2)}, u32[]{:S(2)}) collective-permute-start(f32[4,2,128]{2,1,0:T(2,128)S(1)} %get-tuple-element.27), channel_id=1, source_target_pairs={{0,8},{8,16},{16,24},{1,9},{9,17},{17,25},{2,10},{10,18},{18,26},{... | collective-permute-start | bytes 12296 | tf_op jit(solution)/shard_map/ppermute | solution.py:22
  14.2 3.5 %reshape.94 = f32[4,8,80,2,64]{4,3,2,1,0:T(2,128)S(1)} reshape(bf16[4,8,10240]{2,1,0:T(8,128)(2,1)} %param.6) | data formatting | bytes 1966080 | tf_op jit(solution)/shard_map/convert_element_type | solution.py:89
  18.5 3.8 %multiply_reduce_fusion.4 = f32[4,8,80,64]{3,2,1,0:T(8,128)S(1)} fusion(f32[4,8,80,2,64]{4,3,2,1,0:T(2,128)S(1)} %reshape.94, f32[4,8,2,64]{3,2,1,0:T(2,128)S(1)} %mul.273), kind=kLoop, calls=%fused_computation.7 | loop fusion | flops 491520 | bytes 1982464 | tf_op jit(solution)/shard_map/reduce_sum | solution.py:89
  22.4 3.0 %fusion.8 = f32[80,64,32]{1,2,0:S(1)} fusion(f32[4,8,80,64]{3,2,1,0:T(8,128)S(1)} %multiply_reduce_fusion.4, f32[80]{0:T(128)S(1)} %add_convert_fusion, f32[64,64]{1,0:T(8,128)S(1)} %abs_convert_fusion), kind=kOutput, calls=%fused_computation.18 | convolution fusion | flops 127139840 | bytes 1327424
  25.4 2.8 %convolution_bitcast_fusion.3 = f32[4,8,80,64]{3,1,0,2:T(8,128)S(1)} fusion(f32[80,64,32]{1,2,0:S(1)} %fusion.8, f32[80]{0:T(128)S(1)} %add_convert_fusion, f32[64,64]{1,0:T(8,128)S(1)} %abs_convert_fusion), kind=kOutput, calls=%fused_computation.11 | convolution fusion | flops 127139840 | bytes 1327424
  31.1 2.4 %collective-permute-start.4 = (f32[4,2,128]{2,1,0:T(2,128)S(1)}, f32[4,2,128]{2,1,0:T(2,128)S(1)}, u32[]{:S(2)}, u32[]{:S(2)}) collective-permute-start(f32[4,2,128]{2,1,0:T(2,128)S(1)} %get-tuple-element.31), channel_id=1, source_target_pairs={{0,8},{8,16},{16,24},{24,0},{1,9},{9,17},{17,25},{25,1},{2,10},{10... | collective-permute-start | bytes 12296 | tf_op jit(solution)/shard_map/ppermute | solution.py:22
  37.3 3.5 %collective-permute-start.7 = (f32[2,12,128]{2,1,0:T(8,128)S(1)}, f32[2,12,128]{2,1,0:T(8,128)S(1)}, u32[]{:S(2)}, u32[]{:S(2)}) collective-permute-start(f32[2,12,128]{2,1,0:T(8,128)S(1)} %get-tuple-element.26), channel_id=1, source_target_pairs={{1,0},{2,1},{3,2},{4,3},{5,4},{6,5},{7,6},{0,7},{9,8},{10,9},{11,1... | collective-permute-start | bytes 36872 | tf_op jit(solution)/shard_map/ppermute | solution.py:25
  42.7 3.6 %collective-permute-start.9 = (f32[3,16,128]{2,1,0:T(8,128)S(1)}, f32[3,16,128]{2,1,0:T(8,128)S(1)}, u32[]{:S(2)}, u32[]{:S(2)}) collective-permute-start(f32[3,16,128]{2,1,0:T(8,128)S(1)} %get-tuple-element.14), channel_id=1, source_target_pairs={{1,0},{2,1},{3,2},{4,3},{5,4},{6,5},{7,6},{0,7},{9,8},{10,9},{11,1... | collective-permute-start | bytes 73736 | tf_op jit(solution)/shard_map/ppermute | solution.py:25
  48.0 4.8 %collective-permute-start.10 = (f32[4,2,128]{2,1,0:T(2,128)S(1)}, f32[4,2,128]{2,1,0:T(2,128)S(1)}, u32[]{:S(2)}, u32[]{:S(2)}) collective-permute-start(f32[4,2,128]{2,1,0:T(2,128)S(1)} %get-tuple-element.23), channel_id=1, source_target_pairs={{0,8},{8,16},{16,24},{1,9},{9,17},{17,25},{2,10},{10,18},{18,26},{... | collective-permute-start | bytes 12296 | tf_op jit(solution)/shard_map/ppermute | solution.py:22
  54.1 4.2 %collective-permute-done.11 = f32[4,2,128]{2,1,0:T(2,128)S(1)} collective-permute-done((f32[4,2,128]{2,1,0:T(2,128)S(1)}, f32[4,2,128]{2,1,0:T(2,128)S(1)}, u32[]{:S(2)}, u32[]{:S(2)}) %collective-permute-start.11) | collective-permute-done | bytes 4128 | tf_op jit(solution)/shard_map/ppermute | solution.py:25
  58.5 3.8 %multiply_reduce_fusion.2 = f32[4,8,80,64]{3,2,1,0:T(8,128)S(1)} fusion(f32[4,8,80,2,64]{4,3,2,1,0:T(2,128)S(1)} %reshape.94, f32[4,8,2,64]{3,2,1,0:T(2,128)S(1)} %mul.296), kind=kLoop, calls=%fused_computation.5 | loop fusion | flops 491520 | bytes 1982464 | tf_op jit(solution)/shard_map/reduce_sum | solution.py:89
  62.4 4.8 %fusion.10 = (f32[]{:T(128)}, f32[]{:T(128)}, f32[4,8,80,64]{3,1,0,2:T(8,128)}) fusion(f32[80,64,32]{1,2,0:S(1)} %copy-done.1, f32[4,8,80,64]{3,2,1,0:T(8,128)S(1)} %multiply_reduce_fusion.2, f32[80]{0:T(128)S(1)} %add_convert_fusion, f32[64,64]{1,0:T(8,128)S(1)} %abs_convert_fusion), kind=kOutput, calls=%fused_computation.23 | convolution fusion | flops 127959040 | bytes 1982792
  68.5 15.7 %psum.28 = f32[2]{0:T(128)S(1)} all-reduce(f32[2]{0:T(128)S(1)} %pad_maximum_fusion.8), channel_id=1, replica_groups=mesh['lat'=4,'lon'=8] {'lon'}, use_global_device_ids=true, to_apply=%region_5.6 | all-reduce | flops 2 | bytes 16 | tf_op jit(solution)/shard_map/psum | solution.py:134
  84.2 8.8 %psum.29 = f32[2]{0:T(128)S(1)} all-reduce(f32[2]{0:T(128)S(1)} %psum.28), channel_id=1, replica_groups=mesh['lat'=4,'lon'=8] {'lat'}, use_global_device_ids=true, to_apply=%region_6.7 | all-reduce | flops 2 | bytes 16 | tf_op jit(solution)/shard_map/psum | solution.py:134
  94.9 4.7 %convolution_bitcast_fusion.1 = f32[4,8,80,64]{3,1,0,2:T(8,128)S(1)} fusion(f32[80]{0:T(128)S(1)} %add_convert_fusion, f32[64,64]{1,0:T(8,128)S(1)} %abs_convert_fusion, f32[4,8,80,64]{3,1,0,2:T(8,128)} %get-tuple-element.38, f32[]{:T(128)} %bitcast.25, f32[]{:T(128)} %bitcast.23, f32[80,64,32]{1,2,0} %copy-done), kind=kOutput, calls=%fused_computation.9 | convolution fusion | flops 127795200 | bytes 1982792
  106.7 3.5 %collective-permute-start.15 = (f32[2,12,128]{2,1,0:T(8,128)S(1)}, f32[2,12,128]{2,1,0:T(8,128)S(1)}, u32[]{:S(2)}, u32[]{:S(2)}) collective-permute-start(f32[2,12,128]{2,1,0:T(8,128)S(1)} %get-tuple-element.22), channel_id=1, source_target_pairs={{1,0},{2,1},{3,2},{4,3},{5,4},{6,5},{7,6},{0,7},{9,8},{10,9},{11,1... | collective-permute-start | bytes 36872 | tf_op jit(solution)/shard_map/ppermute | solution.py:25
  112.1 3.6 %collective-permute-start.17 = (f32[3,16,128]{2,1,0:T(8,128)S(1)}, f32[3,16,128]{2,1,0:T(8,128)S(1)}, u32[]{:S(2)}, u32[]{:S(2)}) collective-permute-start(f32[3,16,128]{2,1,0:T(8,128)S(1)} %get-tuple-element.10), channel_id=1, source_target_pairs={{1,0},{2,1},{3,2},{4,3},{5,4},{6,5},{7,6},{0,7},{9,8},{10,9},{11,1... | collective-permute-start | bytes 73736 | tf_op jit(solution)/shard_map/ppermute | solution.py:25
  117.4 4.8 %collective-permute-start.18 = (f32[4,2,128]{2,1,0:T(2,128)S(1)}, f32[4,2,128]{2,1,0:T(2,128)S(1)}, u32[]{:S(2)}, u32[]{:S(2)}) collective-permute-start(f32[4,2,128]{2,1,0:T(2,128)S(1)} %get-tuple-element.19), channel_id=1, source_target_pairs={{0,8},{8,16},{16,24},{1,9},{9,17},{17,25},{2,10},{10,18},{18,26},{... | collective-permute-start | bytes 12296 | tf_op jit(solution)/shard_map/ppermute | solution.py:22
  123.7 4.0 %collective-permute-done.19 = f32[4,2,128]{2,1,0:T(2,128)S(1)} collective-permute-done((f32[4,2,128]{2,1,0:T(2,128)S(1)}, f32[4,2,128]{2,1,0:T(2,128)S(1)}, u32[]{:S(2)}, u32[]{:S(2)}) %collective-permute-start.19) | collective-permute-done | bytes 4128 | tf_op jit(solution)/shard_map/ppermute | solution.py:25
  127.8 3.8 %multiply_reduce_fusion = f32[4,8,80,64]{3,2,1,0:T(8,128)S(1)} fusion(f32[4,8,80,2,64]{4,3,2,1,0:T(2,128)S(1)} %reshape.94, f32[4,8,2,64]{3,2,1,0:T(2,128)S(1)} %mul.324), kind=kLoop, calls=%fused_computation.3 | loop fusion | flops 491520 | bytes 1982464 | tf_op jit(solution)/shard_map/reduce_sum | solution.py:89
  131.7 5.1 %multiply_reduce_fusion.7 = (f32[]{:T(128)}, f32[]{:T(128)}, f32[]{:T(128)}, f32[4,8,80,64]{3,1,0,2:T(8,128)}) fusion(f32[]{:T(128)} %bitcast.23, f32[80,64,32]{1,2,0:S(1)} %copy-done.2, f32[4,8,80,64]{3,2,1,0:T(8,128)S(1)} %multiply_reduce_fusion, f32[80]{0:T(128)S(1)} %add_convert_fusion, f32[64,64]{1,0:T(8,128)S(1)} %abs_convert_fusion, f32[]{:T(128)} %bitcast.25, ...), kind=kOutput, calls=%fused_computation.31 | convolution fusion | flops 128942080 | bytes 2638164
  138.8 15.7 %psum.30 = f32[3]{0:T(128)S(1)} all-reduce(f32[3]{0:T(128)S(1)} %pad_maximum_fusion.9), channel_id=1, replica_groups=mesh['lat'=4,'lon'=8] {'lon'}, use_global_device_ids=true, to_apply=%region_12.13 | all-reduce | flops 3 | bytes 24 | tf_op jit(solution)/shard_map/psum | solution.py:134
  154.4 8.6 %psum.31 = f32[3]{0:T(128)S(1)} all-reduce(f32[3]{0:T(128)S(1)} %psum.30), channel_id=1, replica_groups=mesh['lat'=4,'lon'=8] {'lat'}, use_global_device_ids=true, to_apply=%region_13.14 | all-reduce | flops 3 | bytes 24 | tf_op jit(solution)/shard_map/psum | solution.py:134
  (100 shorter events, 38.9 us)
Async XLA Ops:
  1.5 6.6 %collective-permute-start = (f32[3,16,128]{2,1,0:T(8,128)S(1)}, f32[3,16,128]{2,1,0:T(8,128)S(1)}, u32[]{:S(2)}, u32[]{:S(2)}) collective-permute-start(f32[3,16,128]{2,1,0:T(8,128)S(1)} %get-tuple-element.17), channel_id=1, source_target_pairs={{0,1},{1,2},{2,3},{3,4},{4,5},{5,6},{6,7},{7,0},{8,9},{9,10},{10,1... | collective-permute-start | bytes 73736 | tf_op jit(solution)/shard_map/ppermute | solution.py:22
  2.1 6.1 %collective-permute-start.1 = (f32[3,16,128]{2,1,0:T(8,128)S(1)}, f32[3,16,128]{2,1,0:T(8,128)S(1)}, u32[]{:S(2)}, u32[]{:S(2)}) collective-permute-start(f32[3,16,128]{2,1,0:T(8,128)S(1)} %get-tuple-element.18), channel_id=1, source_target_pairs={{1,0},{2,1},{3,2},{4,3},{5,4},{6,5},{7,6},{0,7},{9,8},{10,9},{11,1... | collective-permute-start | bytes 73736 | tf_op jit(solution)/shard_map/ppermute | solution.py:25
  9.0 8.7 %collective-permute-start.2 = (f32[4,2,128]{2,1,0:T(2,128)S(1)}, f32[4,2,128]{2,1,0:T(2,128)S(1)}, u32[]{:S(2)}, u32[]{:S(2)}) collective-permute-start(f32[4,2,128]{2,1,0:T(2,128)S(1)} %get-tuple-element.27), channel_id=1, source_target_pairs={{0,8},{8,16},{16,24},{1,9},{9,17},{17,25},{2,10},{10,18},{18,26},{... | collective-permute-start | bytes 12296 | tf_op jit(solution)/shard_map/ppermute | solution.py:22
  12.9 5.5 %collective-permute-start.3 = (f32[4,2,128]{2,1,0:T(2,128)S(1)}, f32[4,2,128]{2,1,0:T(2,128)S(1)}, u32[]{:S(2)}, u32[]{:S(2)}) collective-permute-start(f32[4,2,128]{2,1,0:T(2,128)S(1)} %get-tuple-element.28), channel_id=1, source_target_pairs={{8,0},{16,8},{24,16},{9,1},{17,9},{25,17},{10,2},{18,10},{26,18},{... | collective-permute-start | bytes 12296 | tf_op jit(solution)/shard_map/ppermute | solution.py:25
  29.0 13.2 %copy-start.6 = (f32[16]{0:T(128)S(1)}, f32[16]{0:T(128)}, u32[]{:S(2)}) copy-start(f32[16]{0:T(128)} %param.10) | copy-start | bytes 196
  29.1 13.6 %copy-start.5 = (f32[8,16,128]{2,1,0:T(8,128)S(1)}, f32[8,16,128]{2,1,0:T(8,128)}, u32[]{:S(2)}) copy-start(f32[8,16,128]{2,1,0:T(8,128)} %param.8) | copy-start | bytes 196612
  31.1 4.6 %collective-permute-start.4 = (f32[4,2,128]{2,1,0:T(2,128)S(1)}, f32[4,2,128]{2,1,0:T(2,128)S(1)}, u32[]{:S(2)}, u32[]{:S(2)}) collective-permute-start(f32[4,2,128]{2,1,0:T(2,128)S(1)} %get-tuple-element.31), channel_id=1, source_target_pairs={{0,8},{8,16},{16,24},{24,0},{1,9},{9,17},{17,25},{25,1},{2,10},{10... | collective-permute-start | bytes 12296 | tf_op jit(solution)/shard_map/ppermute | solution.py:22
  33.6 3.7 %collective-permute-start.5 = (f32[4,2,128]{2,1,0:T(2,128)S(1)}, f32[4,2,128]{2,1,0:T(2,128)S(1)}, u32[]{:S(2)}, u32[]{:S(2)}) collective-permute-start(f32[4,2,128]{2,1,0:T(2,128)S(1)} %get-tuple-element.32), channel_id=1, source_target_pairs={{8,0},{16,8},{24,16},{0,24},{9,1},{17,9},{25,17},{1,25},{10,2},{18... | collective-permute-start | bytes 12296 | tf_op jit(solution)/shard_map/ppermute | solution.py:25
  37.3 5.0 %collective-permute-start.6 = (f32[2,12,128]{2,1,0:T(8,128)S(1)}, f32[2,12,128]{2,1,0:T(8,128)S(1)}, u32[]{:S(2)}, u32[]{:S(2)}) collective-permute-start(f32[2,12,128]{2,1,0:T(8,128)S(1)} %get-tuple-element.25), channel_id=1, source_target_pairs={{0,1},{1,2},{2,3},{3,4},{4,5},{5,6},{6,7},{7,0},{8,9},{9,10},{10,1... | collective-permute-start | bytes 36872 | tf_op jit(solution)/shard_map/ppermute | solution.py:22
  37.3 5.0 %collective-permute-start.7 = (f32[2,12,128]{2,1,0:T(8,128)S(1)}, f32[2,12,128]{2,1,0:T(8,128)S(1)}, u32[]{:S(2)}, u32[]{:S(2)}) collective-permute-start(f32[2,12,128]{2,1,0:T(8,128)S(1)} %get-tuple-element.26), channel_id=1, source_target_pairs={{1,0},{2,1},{3,2},{4,3},{5,4},{6,5},{7,6},{0,7},{9,8},{10,9},{11,1... | collective-permute-start | bytes 36872 | tf_op jit(solution)/shard_map/ppermute | solution.py:25
  42.7 5.1 %collective-permute-start.8 = (f32[3,16,128]{2,1,0:T(8,128)S(1)}, f32[3,16,128]{2,1,0:T(8,128)S(1)}, u32[]{:S(2)}, u32[]{:S(2)}) collective-permute-start(f32[3,16,128]{2,1,0:T(8,128)S(1)} %get-tuple-element.13), channel_id=1, source_target_pairs={{0,1},{1,2},{2,3},{3,4},{4,5},{5,6},{6,7},{7,0},{8,9},{9,10},{10,1... | collective-permute-start | bytes 73736 | tf_op jit(solution)/shard_map/ppermute | solution.py:22
  42.7 5.1 %collective-permute-start.9 = (f32[3,16,128]{2,1,0:T(8,128)S(1)}, f32[3,16,128]{2,1,0:T(8,128)S(1)}, u32[]{:S(2)}, u32[]{:S(2)}) collective-permute-start(f32[3,16,128]{2,1,0:T(8,128)S(1)} %get-tuple-element.14), channel_id=1, source_target_pairs={{1,0},{2,1},{3,2},{4,3},{5,4},{6,5},{7,6},{0,7},{9,8},{10,9},{11,1... | collective-permute-start | bytes 73736 | tf_op jit(solution)/shard_map/ppermute | solution.py:25
  48.0 6.1 %collective-permute-start.10 = (f32[4,2,128]{2,1,0:T(2,128)S(1)}, f32[4,2,128]{2,1,0:T(2,128)S(1)}, u32[]{:S(2)}, u32[]{:S(2)}) collective-permute-start(f32[4,2,128]{2,1,0:T(2,128)S(1)} %get-tuple-element.23), channel_id=1, source_target_pairs={{0,8},{8,16},{16,24},{1,9},{9,17},{17,25},{2,10},{10,18},{18,26},{... | collective-permute-start | bytes 12296 | tf_op jit(solution)/shard_map/ppermute | solution.py:22
  52.8 5.5 %collective-permute-start.11 = (f32[4,2,128]{2,1,0:T(2,128)S(1)}, f32[4,2,128]{2,1,0:T(2,128)S(1)}, u32[]{:S(2)}, u32[]{:S(2)}) collective-permute-start(f32[4,2,128]{2,1,0:T(2,128)S(1)} %get-tuple-element.24), channel_id=1, source_target_pairs={{8,0},{16,8},{24,16},{9,1},{17,9},{25,17},{10,2},{18,10},{26,18},{... | collective-permute-start | bytes 12296 | tf_op jit(solution)/shard_map/ppermute | solution.py:25
  102.0 4.5 %collective-permute-start.12 = (f32[4,2,128]{2,1,0:T(2,128)S(1)}, f32[4,2,128]{2,1,0:T(2,128)S(1)}, u32[]{:S(2)}, u32[]{:S(2)}) collective-permute-start(f32[4,2,128]{2,1,0:T(2,128)S(1)} %get-tuple-element.29), channel_id=1, source_target_pairs={{0,8},{8,16},{16,24},{24,0},{1,9},{9,17},{17,25},{25,1},{2,10},{10... | collective-permute-start | bytes 12296 | tf_op jit(solution)/shard_map/ppermute | solution.py:22
  102.8 3.8 %collective-permute-start.13 = (f32[4,2,128]{2,1,0:T(2,128)S(1)}, f32[4,2,128]{2,1,0:T(2,128)S(1)}, u32[]{:S(2)}, u32[]{:S(2)}) collective-permute-start(f32[4,2,128]{2,1,0:T(2,128)S(1)} %get-tuple-element.30), channel_id=1, source_target_pairs={{8,0},{16,8},{24,16},{0,24},{9,1},{17,9},{25,17},{1,25},{10,2},{18... | collective-permute-start | bytes 12296 | tf_op jit(solution)/shard_map/ppermute | solution.py:25
  106.6 5.0 %collective-permute-start.14 = (f32[2,12,128]{2,1,0:T(8,128)S(1)}, f32[2,12,128]{2,1,0:T(8,128)S(1)}, u32[]{:S(2)}, u32[]{:S(2)}) collective-permute-start(f32[2,12,128]{2,1,0:T(8,128)S(1)} %get-tuple-element.21), channel_id=1, source_target_pairs={{0,1},{1,2},{2,3},{3,4},{4,5},{5,6},{6,7},{7,0},{8,9},{9,10},{10,1... | collective-permute-start | bytes 36872 | tf_op jit(solution)/shard_map/ppermute | solution.py:22
  106.7 5.0 %collective-permute-start.15 = (f32[2,12,128]{2,1,0:T(8,128)S(1)}, f32[2,12,128]{2,1,0:T(8,128)S(1)}, u32[]{:S(2)}, u32[]{:S(2)}) collective-permute-start(f32[2,12,128]{2,1,0:T(8,128)S(1)} %get-tuple-element.22), channel_id=1, source_target_pairs={{1,0},{2,1},{3,2},{4,3},{5,4},{6,5},{7,6},{0,7},{9,8},{10,9},{11,1... | collective-permute-start | bytes 36872 | tf_op jit(solution)/shard_map/ppermute | solution.py:25
  112.0 5.1 %collective-permute-start.16 = (f32[3,16,128]{2,1,0:T(8,128)S(1)}, f32[3,16,128]{2,1,0:T(8,128)S(1)}, u32[]{:S(2)}, u32[]{:S(2)}) collective-permute-start(f32[3,16,128]{2,1,0:T(8,128)S(1)} %get-tuple-element.9), channel_id=1, source_target_pairs={{0,1},{1,2},{2,3},{3,4},{4,5},{5,6},{6,7},{7,0},{8,9},{9,10},{10,1... | collective-permute-start | bytes 73736 | tf_op jit(solution)/shard_map/ppermute | solution.py:22
  112.1 5.1 %collective-permute-start.17 = (f32[3,16,128]{2,1,0:T(8,128)S(1)}, f32[3,16,128]{2,1,0:T(8,128)S(1)}, u32[]{:S(2)}, u32[]{:S(2)}) collective-permute-start(f32[3,16,128]{2,1,0:T(8,128)S(1)} %get-tuple-element.10), channel_id=1, source_target_pairs={{1,0},{2,1},{3,2},{4,3},{5,4},{6,5},{7,6},{0,7},{9,8},{10,9},{11,1... | collective-permute-start | bytes 73736 | tf_op jit(solution)/shard_map/ppermute | solution.py:25
  117.4 6.3 %collective-permute-start.18 = (f32[4,2,128]{2,1,0:T(2,128)S(1)}, f32[4,2,128]{2,1,0:T(2,128)S(1)}, u32[]{:S(2)}, u32[]{:S(2)}) collective-permute-start(f32[4,2,128]{2,1,0:T(2,128)S(1)} %get-tuple-element.19), channel_id=1, source_target_pairs={{0,8},{8,16},{16,24},{1,9},{9,17},{17,25},{2,10},{10,18},{18,26},{... | collective-permute-start | bytes 12296 | tf_op jit(solution)/shard_map/ppermute | solution.py:22
  122.2 5.5 %collective-permute-start.19 = (f32[4,2,128]{2,1,0:T(2,128)S(1)}, f32[4,2,128]{2,1,0:T(2,128)S(1)}, u32[]{:S(2)}, u32[]{:S(2)}) collective-permute-start(f32[4,2,128]{2,1,0:T(2,128)S(1)} %get-tuple-element.20), channel_id=1, source_target_pairs={{8,0},{16,8},{24,16},{9,1},{17,9},{25,17},{10,2},{18,10},{26,18},{... | collective-permute-start | bytes 12296 | tf_op jit(solution)/shard_map/ppermute | solution.py:25
  127.8 3.9 %copy-start.2 = (f32[80,64,32]{1,2,0:S(1)}, f32[80,64,32]{1,2,0}, u32[]{:S(2)}) copy-start(f32[80,64,32]{1,2,0} %copy-done) | copy-start | bytes 1966084
  131.7 34.0 %copy-start.3 = (f32[80,64,32]{1,2,0:S(1)}, f32[80,64,32]{1,2,0}, u32[]{:S(2)}) copy-start(f32[80,64,32]{1,2,0} %copy-done) | copy-start | bytes 1966084
  (3 other events, 10.6 us)
